TPU v7x, 256 devices: a whole 4x4x8 slice. The times are simulated.
256 devices in a mesh: ta: 2 (over x_hi), gx: 128 (over x_lo, z, y, core).
Axes of the slice: x: 4 (x_hi: 2, x_lo: 2; x = x_hi * 2 + x_lo), y: 4, z: 8, core: 2. Of those that a mesh axis runs over, the one named last changes fastest.
Arguments:
- voltages: bfloat16 [2, 128, 2, 256, 512], P('ta', 'gx'), may hold values from -6 to 6
- weights: bfloat16 [2, 256, 2, 512, 64], P(None, 'gx'), may hold values from -0.125 to 0.125
Outputs:
- spectra: float32 [256, 2, 512, 64], P(None, None, 'gx', 'ta')
All inputs are finite; a program needn't handle non-finite values.
Results may differ from a plain program's by a relative error of at most 0.0003.
Values may be sent and summed in bfloat16 or wider, within the bound.
A program may use at most 64 MiB of HBM per device.

v0:
```python
import jax
import jax.numpy as jnp
from jax import lax
from jax.sharding import PartitionSpec as P


def split_up(array, dim, devices):
    dims = array.shape
    parts = array.reshape(*dims[:dim], devices, dims[dim] // devices, *dims[dim + 1 :])
    return jnp.moveaxis(parts, dim, 0)


def sum_at_owner(array, axis, dim):
    devices = lax.axis_size(axis)
    parts = lax.all_to_all(split_up(array, dim, devices), axis, 0, 0, tiled=True)
    return jnp.sum(parts, axis=0)


def beam_power(voltage, weight_block):
    antennas = weight_block.shape[3]
    beam_count = weight_block.shape[2]
    powers = []
    for side_index in range(2):
        real_w = weight_block[side_index, 0]
        imag_w = weight_block[side_index, 1]
        upper_rows = jnp.stack([real_w, -imag_w], axis=-1).reshape(beam_count, 2 * antennas)
        bottom_half_rows = jnp.stack([imag_w, real_w], axis=-1).reshape(beam_count, 2 * antennas)
        matrix = jnp.concatenate([upper_rows, bottom_half_rows], 0)
        signal = voltage[side_index * antennas : (side_index + 1) * antennas].reshape(
            2 * antennas, -1
        )
        beam_voltage_field = jnp.dot(matrix, signal, preferred_element_type=jnp.float32)
        power = (
            beam_voltage_field[:beam_count] * beam_voltage_field[:beam_count]
            + beam_voltage_field[beam_count:] * beam_voltage_field[beam_count:]
        )
        powers.append(power.reshape(beam_count, -1, 8).sum(-1))
    return jnp.stack(powers, 0)


def channel_powers(turned, weights):

    def one_channel(column):
        voltage = lax.dynamic_index_in_dim(turned, column, 2, keepdims=False)
        weight_block = lax.dynamic_index_in_dim(weights, column, 1, keepdims=False)
        return beam_power(voltage, weight_block)

    return lax.map(one_channel, jnp.arange(turned.shape[2], dtype=jnp.int32))


def on_device(voltages, weights):
    turned = lax.all_to_all(voltages, "gx", split_axis=3, concat_axis=1, tiled=True)
    partial_power_value = channel_powers(turned[0], weights)
    summed = jax.tree.map(lambda part: sum_at_owner(part, "ta", 3), partial_power_value)
    return lax.all_to_all(summed, "gx", split_axis=2, concat_axis=0, tiled=True)


def solution(mesh):
    in_specs = (P("ta", "gx", None, None, None), P(None, "gx", None, None, None))
    out_specs = P(None, None, "gx", "ta")
    return jax.shard_map(
        on_device, mesh=mesh, in_specs=in_specs, out_specs=out_specs, check_vma=False
    )
```

profile of v0, /device:TPU:1, one launch (start us, length us, event | category | flops | bytes accessed | tf_op | source)
XLA Modules:
  0.0 90.3 jit_solution(15072993116613332822)
XLA Ops:
  0.0 2.4 %copy.25 = bf16[1,1,2,256,512]{4,2,1,0,3:T(2,128)(2,1)} copy(bf16[1,1,2,256,512]{4,3,2,1,0:T(8,128)(2,1)} %param.4) | data formatting | bytes 1048576 | tf_op args[0]
  2.4 14.9 %all-to-all-start = ((bf16[1,1,2,256,512]{4,2,1,0,3:T(2,128)(2,1)}), bf16[1,1,2,256,512]{4,2,1,0,3:T(2,128)(2,1)S(1)}, u32[]{:S(2)}, u32[]{:S(2)}) async-start(bf16[1,1,2,256,512]{4,2,1,0,3:T(2,128)(2,1)} %copy.25), calls=%async_computation | async-start | bytes 1048576 | tf_op jit(solution)/shard_map/all_to_all | solution.py:52
  17.3 20.5 %all-to-all-done = bf16[1,1,2,256,512]{4,2,1,0,3:T(2,128)(2,1)S(1)} async-done(((bf16[1,1,2,256,512]{4,2,1,0,3:T(2,128)(2,1)}), bf16[1,1,2,256,512]{4,2,1,0,3:T(2,128)(2,1)S(1)}, u32[]{:S(2)}, u32[]{:S(2)}) %all-to-all-start) | async-done | bytes 524320 | tf_op jit(solution)/shard_map/all_to_all | solution.py:52
  37.8 12.3 %while.10 = (s32[]{:T(128)}, f32[2,2,512,64]{2,3,1,0:T(8,128)S(1)}, s32[2]{0:T(128)S(1)}, bf16[2,2,2,512,64]{3,4,2,1,0:T(8,128)(2,1)S(1)}, bf16[128,2,2,512]{3,1...) while((s32[]{:T(128)}, f32[2,2,512,64]{2,3,1,0:T(8,128)S(1)}, s32[2]{0:T(128)S(1)}, ...), condition=%wide.region_3.4_spmd, body=%wide.region_0.3_spmd.sunk | while | flops 271908864 | bytes 15859855 | solution.py:48
  37.8 0.7 dynamic_slice.19
  40.7 0.1 copy.43
  40.8 0.1 reshape.65
  40.9 0.1 copy.44
  41.0 0.1 reshape.66
  41.1 0.2 dynamic-slice_bitcast_fusion.4
  41.3 0.2 fusion.37
  41.5 0.1 reshape.64
  41.6 0.5 fusion.41
  42.0 0.5 fusion.42
  42.5 0.1 copy.41
  42.7 0.1 reshape.62
  42.7 0.1 copy.42
  42.9 0.1 reshape.63
  42.9 0.1 reshape.61
  43.0 0.5 fusion.39
  43.5 0.5 fusion.40
  44.0 0.7 dynamic_slice.19
  46.9 0.1 copy.43
  47.0 0.1 reshape.65
  47.1 0.1 copy.44
  47.2 0.1 reshape.66
  47.3 0.2 dynamic-slice_bitcast_fusion.4
  47.5 0.2 fusion.37
  47.7 0.1 reshape.64
  47.7 0.5 fusion.41
  48.2 0.5 fusion.42
  48.7 0.1 copy.41
  48.8 0.1 reshape.62
  48.9 0.1 copy.42
  49.0 0.1 reshape.63
  49.1 0.1 reshape.61
  49.2 0.5 fusion.39
  49.6 0.5 fusion.40
  50.2 12.5 %all_to_all.38 = f32[2,2,2,512,32]{3,4,2,1,0:T(8,128)S(1)} all-to-all(f32[2,2,2,512,32]{3,4,2,1,0:T(8,128)S(1)} %copy.28), channel_id=1, replica_groups=mesh['ta'=2,'gx'=128] {'ta'}, dimensions={0} | all-to-all | bytes 1048576 | tf_op jit(solution)/shard_map/all_to_all | solution.py:15
  62.7 0.7 copy.30
  63.4 1.0 %reshape.53 = f32[128,1,512]{2,1,0:T(1,128)S(1)} reshape(f32[512,2,2,32]{3,2,1,0:T(2,128)S(1)} %bitcast.88) | data formatting | bytes 524288
  64.5 21.2 %all_to_all.39 = f32[128,1,512]{2,1,0:T(1,128)S(1)} all-to-all(f32[128,1,512]{2,1,0:T(1,128)S(1)} %reshape.53), channel_id=1, replica_groups=mesh['ta'=2,'gx'=128] {'gx'}, dimensions={0} | all-to-all | bytes 524288 | tf_op jit(solution)/shard_map/all_to_all | solution.py:55
  85.7 0.5 broadcast
  86.2 1.3 %reduce = f32[128,512]{1,0:T(8,128)S(1)} reduce(f32[128,1,512]{2,1,0:T(1,128)S(1)} %all_to_all.39, f32[]{:T(128)} %broadcast), dimensions={1}, to_apply=%all_to_all.31.reduce_sub_computation | reduce | bytes 524292 | tf_op jit(solution)/shard_map/all_to_all | solution.py:55
  87.4 0.9 reshape.54
  88.3 0.1 copy.31
  88.4 0.8 copy.32
  89.2 1.0 %copy.33 = f32[256,2,4,32]{0,3,2,1:T(8,128)} copy(f32[256,2,4,32]{3,0,2,1:T(8,128)S(1)} %bitcast.90) | data formatting | bytes 524288 | tf_op jit(solution)/shard_map/all_to_all | solution.py:55
  (16 shorter events, 0.3 us)
Async XLA Ops:
  0.0 37.8 %copy-start = (bf16[2,2,2,512,64]{3,4,2,1,0:T(8,128)(2,1)S(1)}, bf16[2,2,2,512,64]{3,4,2,1,0:T(8,128)(2,1)}, u32[]{:S(2)}) copy-start(bf16[2,2,2,512,64]{3,4,2,1,0:T(8,128)(2,1)} %param.5) | copy-start | bytes 1572868
  2.4 35.4 %all-to-all-start = ((bf16[1,1,2,256,512]{4,2,1,0,3:T(2,128)(2,1)}), bf16[1,1,2,256,512]{4,2,1,0,3:T(2,128)(2,1)S(1)}, u32[]{:S(2)}, u32[]{:S(2)}) async-start(bf16[1,1,2,256,512]{4,2,1,0,3:T(2,128)(2,1)} %copy.25), calls=%async_computation | async-start | bytes 1048576 | tf_op jit(solution)/shard_map/all_to_all | solution.py:52
where the time goes:
time: 90.6 us; the launch traced here: 90.3 us
  blocking collectives  33.7 us (37%)
  waiting for transfers between devices  20.5 us (23%)
  starting transfers between devices  14.9 us (16%)
  local copies, waits for them, and re-layouts  11.5 us (13%)
  loops' own time  4.45 us (5%)
  other arithmetic  3.32 us (4%)
  matrix products  1.9 us (2%)
    all_to_all x1, blocking collectives, on_device(): return lax.all_to_all(summed, 'gx', split_axis=2, concat_axis=0, tiled=True)  21.2 us
    all_to_all x1, waiting for transfers between devices, on_device(): lax.all_to_all(voltages, 'gx', split_axis=3, concat_axis=1, tiled=True)  20.5 us
    all_to_all x1, starting transfers between devices, on_device(): lax.all_to_all(voltages, 'gx', split_axis=3, concat_axis=1, tiled=True)  14.9 us
    all_to_all x1, blocking collectives, sum_at_owner(): lax.all_to_all(split_up(array, dim, devices), axis, 0, 0, tiled=True)  12.5 us
    another operation x1, loops' own time, channel_powers(): return lax.map(one_channel, jnp.arange(turned.shape[2], dtype=jnp.int32))  4.45 us
    unnamed x5, local copies, waits for them, and re-layouts  4.37 us
    all_to_all x4, local copies, waits for them, and re-layouts, on_device(): return lax.all_to_all(summed, 'gx', split_axis=2, concat_axis=0, tiled=True)  2.41 us
    dot_general x4, matrix products, beam_power(): jnp.dot(matrix, signal, preferred_element_type=jnp.float32)  1.9 us
  transfers between devices with their start and end apart: 1, of which 1 were waited for; matrix products, arithmetic and copies ran while one was open for 0% of the time, Pallas kernels for 0%

commit v1 on v0

v1 whole, which is shorter than its diff:
```python
import jax
import jax.numpy as jnp
from jax import lax
from jax.experimental import pallas as pl
from jax.experimental.pallas import tpu as pltpu
from jax.sharding import PartitionSpec as P

MESH = pl.DeviceIdType.MESH
BF = jnp.bfloat16
F32 = jnp.float32
NX, NY, NZ, NC = 4, 4, 8, 2
FAR_Z = (4, 3, 5, 2, 6, 1, 7, 0)


def iota(shape, dim):
    return lax.broadcasted_iota(jnp.int32, shape, dim)


def one_hot(cond):
    return jnp.where(cond, 1.0, 0.0).astype(BF)


def dot(a, b):
    return jnp.dot(a, b, preferred_element_type=F32)


def tn_dot(a, b):
    return lax.dot_general(a, b, (((0,), (0,)), ((), ())), preferred_element_type=F32)


def place():
    ta = lax.axis_index("ta")
    g = lax.axis_index("gx")
    core = lax.rem(g, 2)
    y = lax.rem(lax.div(g, 2), NY)
    z = lax.rem(lax.div(g, 8), NZ)
    x = ta * 2 + lax.div(g, 64)
    return ta, g, x, y, z, core


def exchange_kernel(x_hbm, w_hbm, out_ref, xv, wv, snd, rcv, amat, acc, snd2, rcv2,
                    in_sem, send_sem, recv_sem, send2_sem, recv2_sem):
    ta, g, x, y, z, core = place()
    me = ta * 128 + g
    copy_x = pltpu.make_async_copy(x_hbm, xv, in_sem.at[0])
    copy_w = pltpu.make_async_copy(w_hbm, wv, in_sem.at[1])
    copy_x.start()
    copy_w.start()

    zs = [lax.rem(z + d, NZ) * 8 for d in range(NZ)]
    cores = [core, 1 - core]

    def xy_of(i):
        dx = lax.rem(lax.div(i, 4) + 2, NX)
        dy = lax.rem(i + 2, NY)
        nx = lax.rem(x + dx, NX)
        ny = lax.rem(y + dy, NY)
        return lax.div(nx, 2), lax.rem(nx, 2) * 64 + ny * 2

    def targets(i, skip_self):
        nta, base = xy_of(i)
        for dz in FAR_Z:
            for dc in range(NC):
                if skip_self and dz == 0 and dc == 0:
                    continue
                yield nta, base + zs[dz] + cores[dc]

    barrier = pltpu.get_barrier_semaphore()

    def greet(nta, ng):
        pl.semaphore_signal(barrier, inc=1, device_id={"ta": nta, "gx": ng}, device_id_type=MESH)

    def greet_step(i, carry):
        for nta, ng in targets(i, False):
            greet(nta, ng)
        return carry

    lax.fori_loop(0, 10, greet_step, 0)
    lax.fori_loop(11, 16, greet_step, 0)
    for nta, ng in targets(10, True):
        greet(nta, ng)

    copy_x.wait()
    r_i, r_k = iota((128, 128), 0), iota((128, 128), 1)
    rows = one_hot(r_k == ((r_i >> 1) & 1) * 64 + (r_i >> 2) * 2 + (r_i & 1))
    p_i, p_k = iota((256, 256), 0), iota((256, 256), 1)
    lanes = one_hot(p_i == (p_k & 31) * 8 + (p_k >> 5))
    snd_rows = snd.reshape(1024, 256)
    for blk in range(4):
        block = jnp.concatenate([xv[0, blk * 64:(blk + 1) * 64], xv[1, blk * 64:(blk + 1) * 64]], 0)
        grouped = dot(rows, block).astype(BF)
        for h in range(2):
            piece = dot(grouped[:, h * 256:(h + 1) * 256], lanes).astype(BF)
            snd_rows[pl.ds(h * 512 + blk * 128, 128), :] = piece

    pl.semaphore_wait(barrier, 255)

    def send(nta, ng):
        pltpu.make_async_remote_copy(
            snd.at[nta * 128 + ng], rcv.at[me], send_sem, recv_sem,
            device_id={"ta": nta, "gx": ng}, device_id_type=MESH).start()

    def send_step(i, carry):
        for nta, ng in targets(i, False):
            send(nta, ng)
        return carry

    lax.fori_loop(0, 10, send_step, 0)
    lax.fori_loop(11, 16, send_step, 0)
    for nta, ng in targets(10, True):
        send(nta, ng)
    rcv[me] = snd[me]

    copy_w.wait()
    e_i, e_k = iota((128, 512), 0), iota((128, 512), 1)
    e_ri, e_a = e_i >> 6, e_i & 63
    k_c, k_a, k_ri, k_j = e_k >> 8, (e_k >> 2) & 63, (e_k >> 1) & 1, e_k & 1
    same = e_a == k_a
    sign = jnp.where((k_c == 0) & (k_ri == 1), -1.0, 1.0)
    for j in range(2):
        spread = jnp.where(same & (e_ri == (k_c ^ k_ri)) & (k_j == j), sign, 0.0).astype(BF)
        for q in range(2):
            both = wv[q, j].reshape(128, 512)
            made = tn_dot(both, spread).astype(BF)
            amat[j * 2 + q, 0:512, :] = made[:, 0:256]
            amat[j * 2 + q, 512:1024, :] = made[:, 256:512]

    pltpu.make_async_copy(snd.at[pl.ds(0, 255)], rcv.at[pl.ds(0, 255)], recv_sem).wait()

    rcv_rows = rcv.reshape(1024, 256)

    def channel(i, carry):
        q = lax.rem(i, 2)
        total = None
        for h in range(2):
            signal = rcv_rows[pl.ds(pl.multiple_of(h * 512 + q * 256, 256), 256), :]
            field = dot(amat[i], signal)
            re, im = field[0:512], field[512:1024]
            power = re * re + im * im
            part = power[:, 0:128] + power[:, 128:256]
            total = part if total is None else total + part
        acc[i] = total
        return carry

    lax.fori_loop(0, 4, channel, 0)

    lane = iota((512, 128), 1)
    low, even = lane < 64, (lane & 32) == 0
    fold = []
    for i in range(2):
        a, b = acc[i], acc[i + 2]
        fold.append(jnp.where(low, a, b) + pltpu.roll(jnp.where(low, b, a), 64, 1))
    other = jnp.where(even, fold[1], fold[0])
    summed = jnp.where(even, fold[0], fold[1]) + jnp.where(
        even, pltpu.roll(other, 96, 1), pltpu.roll(other, 32, 1))
    snd2.reshape(512, 128)[...] = summed

    def send2(ng):
        pltpu.make_async_remote_copy(
            snd2.at[ng], rcv2.at[g], send2_sem, recv2_sem,
            device_id={"ta": ta, "gx": ng}, device_id_type=MESH).start()

    x_lo = lax.div(g, 64)

    def send2_step(i, carry):
        base = lax.rem(x_lo + lax.div(i, 4), 2) * 64 + lax.rem(y + i + 1, NY) * 2
        for dz in FAR_Z:
            for dc in range(NC):
                send2(base + zs[dz] + cores[dc])
        return carry

    lax.fori_loop(0, 3, send2_step, 0)
    lax.fori_loop(4, 8, send2_step, 0)
    base = x_lo * 64 + y * 2
    for dz in FAR_Z:
        for dc in range(NC):
            if dz or dc:
                send2(base + zs[dz] + cores[dc])
    rcv2[g] = snd2[g]
    pltpu.make_async_copy(snd2.at[pl.ds(0, 127)], rcv2.at[pl.ds(0, 127)], recv2_sem).wait()
    out_ref[...] = rcv2[...]
    pltpu.make_async_copy(snd.at[pl.ds(0, 255)], rcv.at[pl.ds(0, 255)], send_sem).wait()
    pltpu.make_async_copy(snd2.at[pl.ds(0, 127)], rcv2.at[pl.ds(0, 127)], send2_sem).wait()


def layout_kernel(r_ref, out_ref):
    lane = iota((32, 128), 1)
    half = lane >> 1
    odd = (lane & 1) == 1
    for b in range(4):
        turned = r_ref[:, b, :].T
        for q in range(2):
            first = turned[q * 32:(q + 1) * 32]
            second = turned[64 + q * 32:64 + (q + 1) * 32]
            for part in range(2):
                index = half + part * 64
                out_ref[q, b, :, part * 128:(part + 1) * 128] = jnp.where(
                    odd, jnp.take_along_axis(second, index, axis=1),
                    jnp.take_along_axis(first, index, axis=1))


def solution(mesh):
    def on_device(voltages, weights):
        vmem = pl.BlockSpec(memory_space=pltpu.VMEM)
        hbm = pl.BlockSpec(memory_space=pl.ANY)
        got = pl.pallas_call(
            exchange_kernel,
            out_shape=jax.ShapeDtypeStruct((128, 4, 128), F32),
            in_specs=[hbm, hbm],
            out_specs=vmem,
            scratch_shapes=[
                pltpu.VMEM((2, 256, 512), BF),
                pltpu.VMEM((2, 2, 2, 64, 512), BF),
                pltpu.VMEM((256, 4, 256), BF),
                pltpu.VMEM((256, 4, 256), BF),
                pltpu.VMEM((4, 1024, 256), BF),
                pltpu.VMEM((4, 512, 128), F32),
                pltpu.VMEM((128, 4, 128), F32),
                pltpu.VMEM((128, 4, 128), F32),
                pltpu.SemaphoreType.DMA((2,)),
                pltpu.SemaphoreType.DMA,
                pltpu.SemaphoreType.DMA,
                pltpu.SemaphoreType.DMA,
                pltpu.SemaphoreType.DMA,
            ],
            compiler_params=pltpu.CompilerParams(collective_id=0, has_side_effects=True),
        )(voltages[0, 0], jnp.swapaxes(weights, 3, 4))
        out = pl.pallas_call(
            layout_kernel,
            out_shape=jax.ShapeDtypeStruct((2, 4, 32, 256), F32),
            in_specs=[vmem],
            out_specs=vmem,
        )(got)
        return jnp.transpose(out, (3, 0, 1, 2))

    return jax.shard_map(
        on_device,
        mesh=mesh,
        in_specs=(P("ta", "gx", None, None, None), P(None, "gx", None, None, None)),
        out_specs=P(None, None, "gx", "ta"),
        check_vma=False,
    )
```

time: 90.6 us -> 44.1 us (0.49)
  Pallas kernels: 0 us -> 44 us
  blocking collectives: 33.7 us -> 0 us
  waiting for transfers between devices: 20.5 us -> 0 us
  starting transfers between devices: 14.9 us -> 0 us
  local copies, waits for them, and re-layouts: 11.5 us -> 0 us
  loops' own time: 4.45 us -> 0 us
  other arithmetic: 3.32 us -> 0 us
  matrix products: 1.9 us -> 0 us
    pallas_call x0 -> x2, Pallas kernels: none -> 44 us  [the longest x1 41.9 us: on_device(): pl.pallas_call(exchange_kernel, out_shape=jax.ShapeDtypeStruct((128, 4, 1...]
    all_to_all x2 -> x0, blocking collectives: 33.7 us -> none  [the longest x1 21.2 us: on_device(): return lax.all_to_all(summed, 'gx', split_axis=2, concat_axis=0, tiled=True)]
    all_to_all x1 -> x0, waiting for transfers between devices: 20.5 us -> none  [on_device(): lax.all_to_all(voltages, 'gx', split_axis=3, concat_axis=1, tiled=True)]
    all_to_all x1 -> x0, starting transfers between devices: 14.9 us -> none  [on_device(): lax.all_to_all(voltages, 'gx', split_axis=3, concat_axis=1, tiled=True)]
    another operation x1 -> x0, loops' own time: 4.45 us -> none  [channel_powers(): return lax.map(one_channel, jnp.arange(turned.shape[2], dtype=jnp.int32))]
    unnamed x5 -> x0, local copies, waits for them, and re-layouts: 4.37 us -> none
    all_to_all x4 -> x0, local copies, waits for them, and re-layouts: 2.41 us -> none  [on_device(): return lax.all_to_all(summed, 'gx', split_axis=2, concat_axis=0, tiled=True)]
    reduce_sum x5 -> x0, other arithmetic: 1.91 us -> none  [the longest x4 1.87 us: beam_power(): powers.append(power.reshape(beam_count, -1, 8).sum(-1))]
  transfers between devices with their start and end apart: 1 -> 0, of which waited for: 1 -> 0; matrix products, arithmetic and copies ran while one was open for 0% -> 0% of each run, Pallas kernels for 0% -> 0%
where the time goes in v1:
time: 44.1 us; the launch traced here: 44 us
  Pallas kernels  44 us (100%)
    pallas_call x1, Pallas kernels, on_device(): pl.pallas_call(exchange_kernel, out_shape=jax.ShapeDtypeStruct((128, 4, 1...  41.9 us
    pallas_call x1, Pallas kernels, on_device(): pl.pallas_call(layout_kernel, out_shape=jax.ShapeDtypeStruct((2, 4, 32, 2...  2.06 us

profile of v1, /device:TPU:1, one launch (start us, length us, event | category | flops | bytes accessed | tf_op | source)
XLA Modules:
  0.0 44.0 jit_solution(16406603369640426736)
XLA Ops:
  0.0 41.9 %shard_map.28.r_ref = f32[128,4,128]{2,1,0:T(4,128)} custom-call(bf16[2,256,512]{2,1,0:T(8,128)(2,1)} %bitcast.3, bf16[2,2,2,64,512]{4,3,2,1,0:T(8,128)(2,1)} %bitcast.4), custom_call_target="tpu_custom_call" | custom-call | tf_op jit(solution)/shard_map/pallas_call | solution.py:206
  42.0 2.1 %shard_map.29 = f32[2,4,32,256]{3,2,1,0:T(8,128)} custom-call(f32[128,4,128]{2,1,0:T(4,128)} %shard_map.28.r_ref), custom_call_target="tpu_custom_call" | custom-call | tf_op jit(solution)/shard_map/pallas_call | solution.py:228

commit v2 on v1

v2 whole, which is shorter than its diff:
```python
import jax
import jax.numpy as jnp
from jax import lax
from jax.experimental import pallas as pl
from jax.experimental.pallas import tpu as pltpu
from jax.sharding import PartitionSpec as P

MESH = pl.DeviceIdType.MESH
BF = jnp.bfloat16
F32 = jnp.float32
NX, NY, NZ, NC = 4, 4, 8, 2


def iota(shape, dim):
    return lax.broadcasted_iota(jnp.int32, shape, dim)


def one_hot(cond):
    return jnp.where(cond, 1.0, 0.0).astype(BF)


def dot(a, b):
    return jnp.dot(a, b, preferred_element_type=F32)


def tn_dot(a, b):
    return lax.dot_general(a, b, (((0,), (0,)), ((), ())), preferred_element_type=F32)


def exchange_kernel(x_hbm, w_hbm, out_ref, xv, wv, snd, rcv, amat, acc, snd2, rcv2,
                    plane_sem, in_sem, send_sem, recv_sem, send2_sem, recv2_sem):
    ta = lax.axis_index("ta")
    g = lax.axis_index("gx")
    core = lax.rem(g, 2)
    y = lax.rem(lax.div(g, 2), NY)
    z = lax.rem(lax.div(g, 8), NZ)
    x_lo = lax.div(g, 64)
    x = ta * 2 + x_lo
    me = ta * 128 + g
    copy_x = pltpu.make_async_copy(x_hbm, xv, in_sem.at[0])
    copy_w = pltpu.make_async_copy(w_hbm, wv, in_sem.at[1])
    copy_x.start()
    copy_w.start()

    nxs = [lax.rem(x + d, NX) for d in range(NX)]
    tas = [lax.div(v, 2) for v in nxs]
    xbs = [lax.rem(v, 2) * 64 for v in nxs]
    ybs = [lax.rem(y + d, NY) * 2 for d in range(NY)]
    cores = [core, 1 - core]
    plane = [(tas[dx], xbs[dx] + ybs[dy] + cores[dc])
             for dx in (2, 1, 3, 0) for dy in (2, 1, 3, 0) for dc in (1, 0)]

    def signal(sem, nta, ng):
        pl.semaphore_signal(sem, inc=1, device_id={"ta": nta, "gx": ng}, device_id_type=MESH)

    barrier = pltpu.get_barrier_semaphore()
    line = x_lo * 64 + y * 2 + core
    for nta, base in plane[:-1]:
        signal(barrier, nta, base + z * 8)
    for dz in (4, 3, 5, 2, 6, 1, 7):
        signal(barrier, ta, line + lax.rem(z + dz, NZ) * 8)

    copy_x.wait()
    r_i, r_k = iota((128, 128), 0), iota((128, 128), 1)
    rows = one_hot(r_k == (r_i & 1) * 64 + ((r_i >> 1) & 31) * 2 + (r_i >> 6))
    p_i, p_k = iota((256, 256), 0), iota((256, 256), 1)
    lanes = one_hot(p_i == (p_k & 31) * 8 + (p_k >> 5))
    snd_rows = snd.reshape(1024, 256)
    for blk in range(4):
        block = jnp.concatenate([xv[0, blk * 64:(blk + 1) * 64], xv[1, blk * 64:(blk + 1) * 64]], 0)
        grouped = dot(rows, block).astype(BF)
        for h in range(2):
            piece = dot(grouped[:, h * 256:(h + 1) * 256], lanes).astype(BF)
            for j in range(2):
                snd_rows[pl.ds(j * 512 + h * 256 + blk * 64, 64), :] = piece[j * 64:(j + 1) * 64]

    pl.semaphore_wait(barrier, 38)
    for dz in (4, 3, 5, 2, 6, 1, 7):
        signal(plane_sem.at[z], ta, line + lax.rem(z + dz, NZ) * 8)

    def send(j, nta, ng):
        pltpu.make_async_remote_copy(
            snd.at[j * 256 + nta * 128 + ng], rcv.at[j * 256 + me], send_sem.at[j], recv_sem.at[j],
            device_id={"ta": nta, "gx": ng}, device_id_type=MESH).start()

    def send_plane(j, zz):
        for nta, base in plane:
            send(j, nta, base + zz * 8)

    def send_own(j):
        for nta, base in plane[:-1]:
            send(j, nta, base + z * 8)
        rcv[j * 256 + me] = snd[j * 256 + me]

    group = lax.div(z, 4)

    def other_group(i):
        return (1 - group) * 4 + lax.rem(z + i, 4)

    def own_group(i):
        return group * 4 + lax.rem(z + i, 4)

    def wait_and_send(plane_of, j):
        def step(i, carry):
            zz = plane_of(i)
            pl.semaphore_wait(plane_sem.at[zz], 1)
            send_plane(j, zz)
            return carry
        return step

    def just_send(plane_of, j):
        def step(i, carry):
            send_plane(j, plane_of(i))
            return carry
        return step

    lax.fori_loop(1, 4, wait_and_send(own_group, 0), 0)
    send_own(0)
    lax.fori_loop(0, 4, wait_and_send(other_group, 0), 0)
    lax.fori_loop(0, 4, just_send(other_group, 1), 0)
    lax.fori_loop(1, 4, just_send(own_group, 1), 0)
    send_own(1)

    copy_w.wait()
    b_i, b_k = iota((512, 512), 0), iota((512, 512), 1)
    beams = one_hot(b_i == (b_k & 255) * 2 + (b_k >> 8))
    e_i, e_k = iota((128, 256), 0), iota((128, 256), 1)
    e_ri, e_a = e_i >> 6, e_i & 63
    k_c, k_a, k_ri = e_k >> 7, (e_k >> 1) & 63, e_k & 1
    sign = jnp.where((k_c == 0) & (k_ri == 1), -1.0, 1.0)
    spread = jnp.where((e_a == k_a) & (e_ri == (k_c ^ k_ri)), sign, 0.0).astype(BF)
    for j in range(2):
        for q in range(2):
            both = dot(wv[q, j].reshape(128, 512), beams).astype(BF)
            made = tn_dot(both, spread).astype(BF)
            amat[j * 2 + q, 0:512, :] = made[:, 0:128]
            amat[j * 2 + q, 512:1024, :] = made[:, 128:256]

    rcv_rows = rcv.reshape(1024, 256)
    lane = iota((256, 128), 1)
    low, even = lane < 64, (lane & 32) == 0

    def send2(j, ng):
        pltpu.make_async_remote_copy(
            snd2.at[j * 128 + ng], rcv2.at[j * 128 + g], send2_sem.at[j], recv2_sem.at[j],
            device_id={"ta": ta, "gx": ng}, device_id_type=MESH).start()

    half_plane = [lax.rem(x_lo + dx, 2) * 64 + ybs[dy] + cores[dc]
                  for dx in (1, 0) for dy in (2, 1, 3, 0) for dc in (1, 0)]

    for j in range(2):
        pltpu.make_async_copy(snd.at[pl.ds(0, 255)], rcv.at[pl.ds(0, 255)], recv_sem.at[j]).wait()

        def channel(q, carry):
            total = None
            for h in range(2):
                start = pl.multiple_of(j * 512 + h * 256 + q * 128, 128)
                field = dot(amat[j * 2 + q], rcv_rows[pl.ds(start, 128), :])
                re, im = field[0:512], field[512:1024]
                power = re * re + im * im
                part = power[:, 0:128] + power[:, 128:256]
                total = part if total is None else total + part
            acc[q] = total
            return carry

        lax.fori_loop(0, 2, channel, 0)
        fold = []
        for q in range(2):
            a, b = acc[q, 0:256], acc[q, 256:512]
            fold.append(jnp.where(low, a, b) + pltpu.roll(jnp.where(low, b, a), 64, 1))
        other = jnp.where(even, fold[1], fold[0])
        summed = jnp.where(even, fold[0], fold[1]) + jnp.where(
            even, pltpu.roll(other, 96, 1), pltpu.roll(other, 32, 1))
        snd2.reshape(512, 128)[j * 256:(j + 1) * 256, :] = summed

        def send2_step(i, carry):
            zz = lax.rem(z + i, NZ)
            for base in half_plane:
                send2(j, base + zz * 8)
            return carry

        lax.fori_loop(1, NZ, send2_step, 0)
        for base in half_plane[:-1]:
            send2(j, base + z * 8)
        rcv2[j * 128 + g] = snd2[j * 128 + g]

    for j in range(2):
        pltpu.make_async_copy(snd2.at[pl.ds(0, 127)], rcv2.at[pl.ds(0, 127)], recv2_sem.at[j]).wait()
    out_ref[...] = rcv2[...]
    for j in range(2):
        pltpu.make_async_copy(snd.at[pl.ds(0, 255)], rcv.at[pl.ds(0, 255)], send_sem.at[j]).wait()
        pltpu.make_async_copy(snd2.at[pl.ds(0, 127)], rcv2.at[pl.ds(0, 127)], send2_sem.at[j]).wait()


def layout_kernel(r_ref, out_ref):
    lane = iota((32, 128), 1)
    half = lane >> 1
    odd = (lane & 1) == 1
    for high in range(2):
        turned = [r_ref[j * 128:(j + 1) * 128, high, :].T for j in range(2)]
        for parity in range(2):
            for q in range(2):
                at = parity * 64 + q * 32
                for part in range(2):
                    index = half + part * 64
                    out_ref[q, high * 2 + parity, :, part * 128:(part + 1) * 128] = jnp.where(
                        odd, jnp.take_along_axis(turned[1][at:at + 32], index, axis=1),
                        jnp.take_along_axis(turned[0][at:at + 32], index, axis=1))


def solution(mesh):
    def on_device(voltages, weights):
        vmem = pl.BlockSpec(memory_space=pltpu.VMEM)
        hbm = pl.BlockSpec(memory_space=pl.ANY)
        got = pl.pallas_call(
            exchange_kernel,
            out_shape=jax.ShapeDtypeStruct((256, 2, 128), F32),
            in_specs=[hbm, hbm],
            out_specs=vmem,
            scratch_shapes=[
                pltpu.VMEM((2, 256, 512), BF),
                pltpu.VMEM((2, 2, 2, 64, 512), BF),
                pltpu.VMEM((512, 2, 256), BF),
                pltpu.VMEM((512, 2, 256), BF),
                pltpu.VMEM((4, 1024, 128), BF),
                pltpu.VMEM((2, 512, 128), F32),
                pltpu.VMEM((256, 2, 128), F32),
                pltpu.VMEM((256, 2, 128), F32),
                pltpu.SemaphoreType.REGULAR((8,)),
                pltpu.SemaphoreType.DMA((2,)),
                pltpu.SemaphoreType.DMA((2,)),
                pltpu.SemaphoreType.DMA((2,)),
                pltpu.SemaphoreType.DMA((2,)),
                pltpu.SemaphoreType.DMA((2,)),
            ],
            compiler_params=pltpu.CompilerParams(collective_id=0, has_side_effects=True),
        )(voltages[0, 0], jnp.swapaxes(weights, 3, 4))
        out = pl.pallas_call(
            layout_kernel,
            out_shape=jax.ShapeDtypeStruct((2, 4, 32, 256), F32),
            in_specs=[vmem],
            out_specs=vmem,
        )(got)
        return jnp.transpose(out, (3, 0, 1, 2))

    return jax.shard_map(
        on_device,
        mesh=mesh,
        in_specs=(P("ta", "gx", None, None, None), P(None, "gx", None, None, None)),
        out_specs=P(None, None, "gx", "ta"),
        check_vma=False,
    )
```

time: 44.1 us -> 40.8 us (0.925)
  Pallas kernels: 44 us -> 40.7 us
    pallas_call x1, Pallas kernels: 41.9 us -> 38.6 us  [on_device(): pl.pallas_call(exchange_kernel, out_shape=jax.ShapeDtypeStruct((256, 2, 1...]
where the time goes in v2:
time: 40.8 us; the launch traced here: 40.7 us
  Pallas kernels  40.7 us (100%)
    pallas_call x1, Pallas kernels, on_device(): pl.pallas_call(exchange_kernel, out_shape=jax.ShapeDtypeStruct((256, 2, 1...  38.6 us
    pallas_call x1, Pallas kernels, on_device(): pl.pallas_call(layout_kernel, out_shape=jax.ShapeDtypeStruct((2, 4, 32, 2...  2.06 us

profile of v2, /device:TPU:1, one launch (start us, length us, event | category | flops | bytes accessed | tf_op | source)
XLA Modules:
  0.0 40.7 jit_solution(8844519734112753883)
XLA Ops:
  0.0 38.6 %shard_map.28.r_ref = f32[256,2,128]{2,1,0:T(2,128)} custom-call(bf16[2,256,512]{2,1,0:T(8,128)(2,1)} %bitcast.3, bf16[2,2,2,64,512]{4,3,2,1,0:T(8,128)(2,1)} %bitcast.4), custom_call_target="tpu_custom_call" | custom-call | tf_op jit(solution)/shard_map/pallas_call | solution.py:215
  38.7 2.1 %shard_map.29 = f32[2,4,32,256]{3,2,1,0:T(8,128)} custom-call(f32[256,2,128]{2,1,0:T(2,128)} %shard_map.28.r_ref), custom_call_target="tpu_custom_call" | custom-call | tf_op jit(solution)/shard_map/pallas_call | solution.py:238

commit v3 on v2

--- a/solution.py
+++ b/solution.py
@@ -27,8 +27,8 @@
     return lax.dot_general(a, b, (((0,), (0,)), ((), ())), preferred_element_type=F32)
 
 
-def exchange_kernel(x_hbm, w_hbm, out_ref, xv, wv, snd, rcv, amat, acc, snd2, rcv2,
-                    plane_sem, in_sem, send_sem, recv_sem, send2_sem, recv2_sem):
+def exchange_kernel(x_hbm, w_hbm, out_ref, xv, wv, snd, rcv, amat, acc, snd2,
+                    line_sem, in_sem, send_sem, recv_sem, send2_sem, recv2_sem):
     ta = lax.axis_index("ta")
     g = lax.axis_index("gx")
     core = lax.rem(g, 2)
@@ -46,19 +46,21 @@
     tas = [lax.div(v, 2) for v in nxs]
     xbs = [lax.rem(v, 2) * 64 for v in nxs]
     ybs = [lax.rem(y + d, NY) * 2 for d in range(NY)]
+    zbs = [lax.rem(z + d, NZ) * 8 for d in range(NZ)]
     cores = [core, 1 - core]
-    plane = [(tas[dx], xbs[dx] + ybs[dy] + cores[dc])
-             for dx in (2, 1, 3, 0) for dy in (2, 1, 3, 0) for dc in (1, 0)]
+    far_z = (4, 3, 5, 2, 6, 1, 7, 0)
 
     def signal(sem, nta, ng):
         pl.semaphore_signal(sem, inc=1, device_id={"ta": nta, "gx": ng}, device_id_type=MESH)
 
     barrier = pltpu.get_barrier_semaphore()
-    line = x_lo * 64 + y * 2 + core
-    for nta, base in plane[:-1]:
-        signal(barrier, nta, base + z * 8)
-    for dz in (4, 3, 5, 2, 6, 1, 7):
-        signal(barrier, ta, line + lax.rem(z + dz, NZ) * 8)
+    corner = x_lo * 64 + y * 2
+    line = [corner + zbs[dz] + cores[dc] for dz in far_z for dc in (1, 0)]
+    others = [(dx, dy) for dx in (2, 1, 3, 0) for dy in (2, 1, 3, 0)][:-1]
+    for ng in line[:-1]:
+        signal(barrier, ta, ng)
+    for dx, dy in others:
+        signal(barrier, tas[dx], xbs[dx] + ybs[dy] + zbs[0] + core)
 
     copy_x.wait()
     r_i, r_k = iota((128, 128), 0), iota((128, 128), 1)
@@ -74,52 +76,38 @@
             for j in range(2):
                 snd_rows[pl.ds(j * 512 + h * 256 + blk * 64, 64), :] = piece[j * 64:(j + 1) * 64]
 
-    pl.semaphore_wait(barrier, 38)
-    for dz in (4, 3, 5, 2, 6, 1, 7):
-        signal(plane_sem.at[z], ta, line + lax.rem(z + dz, NZ) * 8)
+    pl.semaphore_wait(barrier, 30)
+    for dx, dy in others:
+        signal(line_sem.at[x * 4 + y], tas[dx], xbs[dx] + ybs[dy] + zbs[0] + core)
 
     def send(j, nta, ng):
         pltpu.make_async_remote_copy(
             snd.at[j * 256 + nta * 128 + ng], rcv.at[j * 256 + me], send_sem.at[j], recv_sem.at[j],
             device_id={"ta": nta, "gx": ng}, device_id_type=MESH).start()
 
-    def send_plane(j, zz):
-        for nta, base in plane:
-            send(j, nta, base + zz * 8)
-
     def send_own(j):
-        for nta, base in plane[:-1]:
-            send(j, nta, base + z * 8)
+        for ng in line[:-1]:
+            send(j, ta, ng)
         rcv[j * 256 + me] = snd[j * 256 + me]
 
-    group = lax.div(z, 4)
-
-    def other_group(i):
-        return (1 - group) * 4 + lax.rem(z + i, 4)
-
-    def own_group(i):
-        return group * 4 + lax.rem(z + i, 4)
-
-    def wait_and_send(plane_of, j):
+    def send_line(j, wait):
         def step(i, carry):
-            zz = plane_of(i)
-            pl.semaphore_wait(plane_sem.at[zz], 1)
-            send_plane(j, zz)
+            nx = lax.rem(x + lax.rem(i, NX), NX)
+            ny = lax.rem(y + lax.div(i, NX), NY)
+            if wait:
+                pl.semaphore_wait(line_sem.at[nx * 4 + ny], 1)
+            nta = lax.div(nx, 2)
+            base = lax.rem(nx, 2) * 64 + ny * 2
+            for dz in far_z:
+                for dc in (1, 0):
+                    send(j, nta, base + zbs[dz] + cores[dc])
             return carry
         return step
 
-    def just_send(plane_of, j):
-        def step(i, carry):
-            send_plane(j, plane_of(i))
-            return carry
-        return step
-
-    lax.fori_loop(1, 4, wait_and_send(own_group, 0), 0)
     send_own(0)
-    lax.fori_loop(0, 4, wait_and_send(other_group, 0), 0)
-    lax.fori_loop(0, 4, just_send(other_group, 1), 0)
-    lax.fori_loop(1, 4, just_send(own_group, 1), 0)
+    lax.fori_loop(1, 16, send_line(0, True), 0)
     send_own(1)
+    lax.fori_loop(1, 16, send_line(1, False), 0)
 
     copy_w.wait()
     b_i, b_k = iota((512, 512), 0), iota((512, 512), 1)
@@ -142,7 +130,7 @@
 
     def send2(j, ng):
         pltpu.make_async_remote_copy(
-            snd2.at[j * 128 + ng], rcv2.at[j * 128 + g], send2_sem.at[j], recv2_sem.at[j],
+            snd2.at[j * 128 + ng], out_ref.at[j * 128 + g], send2_sem.at[j], recv2_sem.at[j],
             device_id={"ta": ta, "gx": ng}, device_id_type=MESH).start()
 
     half_plane = [lax.rem(x_lo + dx, 2) * 64 + ybs[dy] + cores[dc]
@@ -174,7 +162,8 @@
         snd2.reshape(512, 128)[j * 256:(j + 1) * 256, :] = summed
 
         def send2_step(i, carry):
-            zz = lax.rem(z + i, NZ)
+            far = 4 + (2 * lax.rem(i, 2) - 1) * lax.div(i, 2)
+            zz = lax.rem(z + far, NZ)
             for base in half_plane:
                 send2(j, base + zz * 8)
             return carry
@@ -182,14 +171,13 @@
         lax.fori_loop(1, NZ, send2_step, 0)
         for base in half_plane[:-1]:
             send2(j, base + z * 8)
-        rcv2[j * 128 + g] = snd2[j * 128 + g]
-
-    for j in range(2):
-        pltpu.make_async_copy(snd2.at[pl.ds(0, 127)], rcv2.at[pl.ds(0, 127)], recv2_sem.at[j]).wait()
-    out_ref[...] = rcv2[...]
+        out_ref[j * 128 + g] = snd2[j * 128 + g]
+
+    for j in range(2):
+        pltpu.make_async_copy(snd2.at[pl.ds(0, 127)], out_ref.at[pl.ds(0, 127)], recv2_sem.at[j]).wait()
     for j in range(2):
         pltpu.make_async_copy(snd.at[pl.ds(0, 255)], rcv.at[pl.ds(0, 255)], send_sem.at[j]).wait()
-        pltpu.make_async_copy(snd2.at[pl.ds(0, 127)], rcv2.at[pl.ds(0, 127)], send2_sem.at[j]).wait()
+        pltpu.make_async_copy(snd2.at[pl.ds(0, 127)], out_ref.at[pl.ds(0, 127)], send2_sem.at[j]).wait()
 
 
 def layout_kernel(r_ref, out_ref):
@@ -214,7 +202,7 @@
         hbm = pl.BlockSpec(memory_space=pl.ANY)
         got = pl.pallas_call(
             exchange_kernel,
-            out_shape=jax.ShapeDtypeStruct((256, 2, 128), F32),
+            out_shape=pltpu.VMEM((256, 2, 128), F32),
             in_specs=[hbm, hbm],
             out_specs=vmem,
             scratch_shapes=[
@@ -225,8 +213,7 @@
                 pltpu.VMEM((4, 1024, 128), BF),
                 pltpu.VMEM((2, 512, 128), F32),
                 pltpu.VMEM((256, 2, 128), F32),
-                pltpu.VMEM((256, 2, 128), F32),
-                pltpu.SemaphoreType.REGULAR((8,)),
+                pltpu.SemaphoreType.REGULAR((16,)),
                 pltpu.SemaphoreType.DMA((2,)),
                 pltpu.SemaphoreType.DMA((2,)),
                 pltpu.SemaphoreType.DMA((2,)),
@@ -240,6 +227,7 @@
             out_shape=jax.ShapeDtypeStruct((2, 4, 32, 256), F32),
             in_specs=[vmem],
             out_specs=vmem,
+            compiler_params=pltpu.CompilerParams(vmem_limit_bytes=8 * 2**20),
         )(got)
         return jnp.transpose(out, (3, 0, 1, 2))
 

time: 40.8 us -> 37.2 us (0.912)
  Pallas kernels: 40.7 us -> 37.1 us
    pallas_call x1, Pallas kernels: 38.6 us -> 36 us  [on_device(): pl.pallas_call(exchange_kernel, out_shape=pltpu.VMEM((256, 2, 128), F32),...]
    pallas_call x1, Pallas kernels: 2.06 us -> 1.11 us  [on_device(): pl.pallas_call(layout_kernel, out_shape=jax.ShapeDtypeStruct((2, 4, 32, 2...]
where the time goes in v3:
time: 37.2 us; the launch traced here: 37.1 us
  Pallas kernels  37.1 us (100%)
    pallas_call x1, Pallas kernels, on_device(): pl.pallas_call(exchange_kernel, out_shape=pltpu.VMEM((256, 2, 128), F32),...  36 us
    pallas_call x1, Pallas kernels, on_device(): pl.pallas_call(layout_kernel, out_shape=jax.ShapeDtypeStruct((2, 4, 32, 2...  1.11 us

profile of v3, /device:TPU:1, one launch (start us, length us, event | category | flops | bytes accessed | tf_op | source)
XLA Modules:
  0.0 37.1 jit_solution(6885607200276685287)
XLA Ops:
  0.0 36.0 %shard_map.28.r_ref = f32[256,2,128]{2,1,0:T(2,128)S(1)} custom-call(bf16[2,256,512]{2,1,0:T(8,128)(2,1)} %bitcast.3, bf16[2,2,2,64,512]{4,3,2,1,0:T(8,128)(2,1)} %bitcast.4), custom_call_target="tpu_custom_call" | custom-call | tf_op jit(solution)/shard_map/pallas_call | solution.py:203
  36.0 1.1 %shard_map.29 = f32[2,4,32,256]{3,2,1,0:T(8,128)} custom-call(f32[256,2,128]{2,1,0:T(2,128)S(1)} %shard_map.28.r_ref), custom_call_target="tpu_custom_call" | custom-call | tf_op jit(solution)/shard_map/pallas_call | solution.py:225

commit v4 on v3

--- a/solution.py
+++ b/solution.py
@@ -92,22 +92,25 @@
 
     def send_line(j, wait):
         def step(i, carry):
-            nx = lax.rem(x + lax.rem(i, NX), NX)
-            ny = lax.rem(y + lax.div(i, NX), NY)
-            if wait:
-                pl.semaphore_wait(line_sem.at[nx * 4 + ny], 1)
-            nta = lax.div(nx, 2)
-            base = lax.rem(nx, 2) * 64 + ny * 2
-            for dz in far_z:
-                for dc in (1, 0):
-                    send(j, nta, base + zbs[dz] + cores[dc])
+            nx = lax.div(i, 8) * 2 + lax.rem(x + i, 2)
+            ny = lax.rem(y + lax.div(lax.rem(i, 8), 2), NY)
+
+            @pl.when((nx != x) | (ny != y))
+            def _():
+                if wait:
+                    pl.semaphore_wait(line_sem.at[nx * 4 + ny], 1)
+                nta = lax.div(nx, 2)
+                base = lax.rem(nx, 2) * 64 + ny * 2
+                for dz in far_z:
+                    for dc in (1, 0):
+                        send(j, nta, base + zbs[dz] + cores[dc])
             return carry
         return step
 
     send_own(0)
-    lax.fori_loop(1, 16, send_line(0, True), 0)
+    lax.fori_loop(0, 16, send_line(0, True), 0)
     send_own(1)
-    lax.fori_loop(1, 16, send_line(1, False), 0)
+    lax.fori_loop(0, 16, send_line(1, False), 0)
 
     copy_w.wait()
     b_i, b_k = iota((512, 512), 0), iota((512, 512), 1)

time: 37.2 us -> 36.1 us (0.970)
  Pallas kernels: 37.1 us -> 36 us
    pallas_call x1, Pallas kernels: 36 us -> 34.9 us  [on_device(): pl.pallas_call(exchange_kernel, out_shape=pltpu.VMEM((256, 2, 128), F32),...]
where the time goes in v4:
time: 36.1 us; the launch traced here: 36 us
  Pallas kernels  36 us (100%)
    pallas_call x1, Pallas kernels, on_device(): pl.pallas_call(exchange_kernel, out_shape=pltpu.VMEM((256, 2, 128), F32),...  34.9 us
    pallas_call x1, Pallas kernels, on_device(): pl.pallas_call(layout_kernel, out_shape=jax.ShapeDtypeStruct((2, 4, 32, 2...  1.11 us

profile of v4, /device:TPU:1, one launch (start us, length us, event | category | flops | bytes accessed | tf_op | source)
XLA Modules:
  0.0 36.0 jit_solution(9873663279471723208)
XLA Ops:
  0.0 34.9 %shard_map.28.r_ref = f32[256,2,128]{2,1,0:T(2,128)S(1)} custom-call(bf16[2,256,512]{2,1,0:T(8,128)(2,1)} %bitcast.3, bf16[2,2,2,64,512]{4,3,2,1,0:T(8,128)(2,1)} %bitcast.4), custom_call_target="tpu_custom_call" | custom-call | tf_op jit(solution)/shard_map/pallas_call | solution.py:206
  34.9 1.1 %shard_map.29 = f32[2,4,32,256]{3,2,1,0:T(8,128)} custom-call(f32[256,2,128]{2,1,0:T(2,128)S(1)} %shard_map.28.r_ref), custom_call_target="tpu_custom_call" | custom-call | tf_op jit(solution)/shard_map/pallas_call | solution.py:228

commit v5 on v4

--- a/solution.py
+++ b/solution.py
@@ -62,27 +62,33 @@
     for dx, dy in others:
         signal(barrier, tas[dx], xbs[dx] + ybs[dy] + zbs[0] + core)
 
-    copy_x.wait()
-    r_i, r_k = iota((128, 128), 0), iota((128, 128), 1)
-    rows = one_hot(r_k == (r_i & 1) * 64 + ((r_i >> 1) & 31) * 2 + (r_i >> 6))
+    r_i, r_k = iota((64, 128), 0), iota((64, 128), 1)
+    picked = (r_i & 1) * 64 + (r_i >> 1) * 2
     p_i, p_k = iota((256, 256), 0), iota((256, 256), 1)
     lanes = one_hot(p_i == (p_k & 31) * 8 + (p_k >> 5))
     snd_rows = snd.reshape(1024, 256)
-    for blk in range(4):
-        block = jnp.concatenate([xv[0, blk * 64:(blk + 1) * 64], xv[1, blk * 64:(blk + 1) * 64]], 0)
-        grouped = dot(rows, block).astype(BF)
+
+    def prepare(j):
+        rows = one_hot(r_k == picked + j)
+        grouped = []
+        for blk in range(4):
+            block = jnp.concatenate([xv[0, blk * 64:(blk + 1) * 64], xv[1, blk * 64:(blk + 1) * 64]], 0)
+            grouped.append(dot(rows, block).astype(BF))
+        grouped = jnp.concatenate(grouped, 0)
         for h in range(2):
-            piece = dot(grouped[:, h * 256:(h + 1) * 256], lanes).astype(BF)
-            for j in range(2):
-                snd_rows[pl.ds(j * 512 + h * 256 + blk * 64, 64), :] = piece[j * 64:(j + 1) * 64]
-
+            snd_rows[j * 512 + h * 256:j * 512 + h * 256 + 256, :] = dot(
+                grouped[:, h * 256:(h + 1) * 256], lanes).astype(BF)
+
+    copy_x.wait()
+    prepare(0)
+    prepare(1)
     pl.semaphore_wait(barrier, 30)
     for dx, dy in others:
         signal(line_sem.at[x * 4 + y], tas[dx], xbs[dx] + ybs[dy] + zbs[0] + core)
 
     def send(j, nta, ng):
         pltpu.make_async_remote_copy(
-            snd.at[j * 256 + nta * 128 + ng], rcv.at[j * 256 + me], send_sem.at[j], recv_sem.at[j],
+            snd.at[j * 256 + nta * 128 + ng], rcv.at[j * 256 + me], send_sem.at[j], recv_sem.at[j * 2 + ta],
             device_id={"ta": nta, "gx": ng}, device_id_type=MESH).start()
 
     def send_own(j):
@@ -140,21 +146,18 @@
                   for dx in (1, 0) for dy in (2, 1, 3, 0) for dc in (1, 0)]
 
     for j in range(2):
-        pltpu.make_async_copy(snd.at[pl.ds(0, 255)], rcv.at[pl.ds(0, 255)], recv_sem.at[j]).wait()
-
-        def channel(q, carry):
-            total = None
-            for h in range(2):
+        for step in range(2):
+            h = ta if step == 0 else 1 - ta
+            n = 127 + step
+            pltpu.make_async_copy(snd.at[pl.ds(0, n)], rcv.at[pl.ds(0, n)], recv_sem.at[j * 2 + h]).wait()
+            for q in range(2):
                 start = pl.multiple_of(j * 512 + h * 256 + q * 128, 128)
                 field = dot(amat[j * 2 + q], rcv_rows[pl.ds(start, 128), :])
                 re, im = field[0:512], field[512:1024]
                 power = re * re + im * im
                 part = power[:, 0:128] + power[:, 128:256]
-                total = part if total is None else total + part
-            acc[q] = total
-            return carry
-
-        lax.fori_loop(0, 2, channel, 0)
+                acc[q] = part if step == 0 else acc[q] + part
+
         fold = []
         for q in range(2):
             a, b = acc[q, 0:256], acc[q, 256:512]
@@ -219,7 +222,7 @@
                 pltpu.SemaphoreType.REGULAR((16,)),
                 pltpu.SemaphoreType.DMA((2,)),
                 pltpu.SemaphoreType.DMA((2,)),
-                pltpu.SemaphoreType.DMA((2,)),
+                pltpu.SemaphoreType.DMA((4,)),
                 pltpu.SemaphoreType.DMA((2,)),
                 pltpu.SemaphoreType.DMA((2,)),
             ],

time: 36.1 us -> 35.9 us (level); the launches traced: 36 us -> 35.4 us
  Pallas kernels: 36 us -> 35.4 us
    pallas_call x1, Pallas kernels: 34.9 us -> 34.3 us  [on_device(): pl.pallas_call(exchange_kernel, out_shape=pltpu.VMEM((256, 2, 128), F32),...]
where the time goes in v5:
time: 35.9 us; the launch traced here: 35.4 us
  Pallas kernels  35.4 us (99%)
    pallas_call x1, Pallas kernels, on_device(): pl.pallas_call(exchange_kernel, out_shape=pltpu.VMEM((256, 2, 128), F32),...  34.3 us
    pallas_call x1, Pallas kernels, on_device(): pl.pallas_call(layout_kernel, out_shape=jax.ShapeDtypeStruct((2, 4, 32, 2...  1.11 us

profile of v5, /device:TPU:1, one launch (start us, length us, event | category | flops | bytes accessed | tf_op | source)
XLA Modules:
  0.0 35.4 jit_solution(10197794754079221383)
XLA Ops:
  0.0 34.3 %shard_map.28.r_ref = f32[256,2,128]{2,1,0:T(2,128)S(1)} custom-call(bf16[2,256,512]{2,1,0:T(8,128)(2,1)} %bitcast.3, bf16[2,2,2,64,512]{4,3,2,1,0:T(8,128)(2,1)} %bitcast.4), custom_call_target="tpu_custom_call" | custom-call | tf_op jit(solution)/shard_map/pallas_call | solution.py:209
  34.3 1.1 %shard_map.29 = f32[2,4,32,256]{3,2,1,0:T(8,128)} custom-call(f32[256,2,128]{2,1,0:T(2,128)S(1)} %shard_map.28.r_ref), custom_call_target="tpu_custom_call" | custom-call | tf_op jit(solution)/shard_map/pallas_call | solution.py:231

commit v6 on v5

--- a/solution.py
+++ b/solution.py
@@ -27,7 +27,7 @@
     return lax.dot_general(a, b, (((0,), (0,)), ((), ())), preferred_element_type=F32)
 
 
-def exchange_kernel(x_hbm, w_hbm, out_ref, xv, wv, snd, rcv, amat, acc, snd2,
+def exchange_kernel(x_hbm, w_hbm, out_ref, xv, wv, snd, rcv, amat, acc, snd2, rcv2,
                     line_sem, in_sem, send_sem, recv_sem, send2_sem, recv2_sem):
     ta = lax.axis_index("ta")
     g = lax.axis_index("gx")
@@ -139,7 +139,7 @@
 
     def send2(j, ng):
         pltpu.make_async_remote_copy(
-            snd2.at[j * 128 + ng], out_ref.at[j * 128 + g], send2_sem.at[j], recv2_sem.at[j],
+            snd2.at[j * 128 + ng], rcv2.at[j * 128 + g], send2_sem.at[j], recv2_sem.at[j],
             device_id={"ta": ta, "gx": ng}, device_id_type=MESH).start()
 
     half_plane = [lax.rem(x_lo + dx, 2) * 64 + ybs[dy] + cores[dc]
@@ -177,29 +177,32 @@
         lax.fori_loop(1, NZ, send2_step, 0)
         for base in half_plane[:-1]:
             send2(j, base + z * 8)
-        out_ref[j * 128 + g] = snd2[j * 128 + g]
-
-    for j in range(2):
-        pltpu.make_async_copy(snd2.at[pl.ds(0, 127)], out_ref.at[pl.ds(0, 127)], recv2_sem.at[j]).wait()
+        rcv2[j * 128 + g] = snd2[j * 128 + g]
+
+    wide = iota((32, 128), 1)
+    odd = (wide & 1) == 1
+
+    def place(j):
+        for high in range(2):
+            turned = rcv2[j * 128:(j + 1) * 128, high, :].T
+            for parity in range(2):
+                for q in range(2):
+                    at = parity * 64 + q * 32
+                    for part in range(2):
+                        cols = slice(part * 128, (part + 1) * 128)
+                        own = jnp.take_along_axis(turned[at:at + 32], (wide >> 1) + part * 64, axis=1)
+                        if j == 0:
+                            out_ref[q, high * 2 + parity, :, cols] = own
+                        else:
+                            out_ref[q, high * 2 + parity, :, cols] = jnp.where(
+                                odd, own, out_ref[q, high * 2 + parity, :, cols])
+
+    for j in range(2):
+        pltpu.make_async_copy(snd2.at[pl.ds(0, 127)], rcv2.at[pl.ds(0, 127)], recv2_sem.at[j]).wait()
+        place(j)
     for j in range(2):
         pltpu.make_async_copy(snd.at[pl.ds(0, 255)], rcv.at[pl.ds(0, 255)], send_sem.at[j]).wait()
-        pltpu.make_async_copy(snd2.at[pl.ds(0, 127)], out_ref.at[pl.ds(0, 127)], send2_sem.at[j]).wait()
-
-
-def layout_kernel(r_ref, out_ref):
-    lane = iota((32, 128), 1)
-    half = lane >> 1
-    odd = (lane & 1) == 1
-    for high in range(2):
-        turned = [r_ref[j * 128:(j + 1) * 128, high, :].T for j in range(2)]
-        for parity in range(2):
-            for q in range(2):
-                at = parity * 64 + q * 32
-                for part in range(2):
-                    index = half + part * 64
-                    out_ref[q, high * 2 + parity, :, part * 128:(part + 1) * 128] = jnp.where(
-                        odd, jnp.take_along_axis(turned[1][at:at + 32], index, axis=1),
-                        jnp.take_along_axis(turned[0][at:at + 32], index, axis=1))
+        pltpu.make_async_copy(snd2.at[pl.ds(0, 127)], rcv2.at[pl.ds(0, 127)], send2_sem.at[j]).wait()
 
 
 def solution(mesh):
@@ -208,7 +211,7 @@
         hbm = pl.BlockSpec(memory_space=pl.ANY)
         got = pl.pallas_call(
             exchange_kernel,
-            out_shape=pltpu.VMEM((256, 2, 128), F32),
+            out_shape=pltpu.VMEM((2, 4, 32, 256), F32),
             in_specs=[hbm, hbm],
             out_specs=vmem,
             scratch_shapes=[
@@ -219,6 +222,7 @@
                 pltpu.VMEM((4, 1024, 128), BF),
                 pltpu.VMEM((2, 512, 128), F32),
                 pltpu.VMEM((256, 2, 128), F32),
+                pltpu.VMEM((256, 2, 128), F32),
                 pltpu.SemaphoreType.REGULAR((16,)),
                 pltpu.SemaphoreType.DMA((2,)),
                 pltpu.SemaphoreType.DMA((2,)),
@@ -228,14 +232,7 @@
             ],
             compiler_params=pltpu.CompilerParams(collective_id=0, has_side_effects=True),
         )(voltages[0, 0], jnp.swapaxes(weights, 3, 4))
-        out = pl.pallas_call(
-            layout_kernel,
-            out_shape=jax.ShapeDtypeStruct((2, 4, 32, 256), F32),
-            in_specs=[vmem],
-            out_specs=vmem,
-            compiler_params=pltpu.CompilerParams(vmem_limit_bytes=8 * 2**20),
-        )(got)
-        return jnp.transpose(out, (3, 0, 1, 2))
+        return jnp.transpose(got, (3, 0, 1, 2))
 
     return jax.shard_map(
         on_device,

time: 35.9 us -> 35.7 us (level)
  Pallas kernels: 35.4 us -> 34.6 us
  local copies, waits for them, and re-layouts: 0 us -> 0.71 us
    pallas_call x2 -> x1, Pallas kernels: 35.4 us -> 34.6 us  [on_device(): pl.pallas_call(exchange_kernel, out_shape=pltpu.VMEM((2, 4, 32, 256), F32...]
    unnamed x0 -> x1, local copies, waits for them, and re-layouts: none -> 0.71 us
where the time goes in v6:
time: 35.7 us; the launch traced here: 35.3 us
  Pallas kernels  34.6 us (97%)
  local copies, waits for them, and re-layouts  0.71 us (2%)
    pallas_call x1, Pallas kernels, on_device(): pl.pallas_call(exchange_kernel, out_shape=pltpu.VMEM((2, 4, 32, 256), F32...  34.6 us

profile of v6, /device:TPU:1, one launch (start us, length us, event | category | flops | bytes accessed | tf_op | source)
XLA Modules:
  0.0 35.3 jit_solution(9466380662051722538)
XLA Ops:
  0.0 34.6 %shard_map.28 = f32[2,4,32,256]{3,2,1,0:T(8,128)S(1)} custom-call(bf16[2,256,512]{2,1,0:T(8,128)(2,1)} %bitcast.4, bf16[2,2,2,64,512]{4,3,2,1,0:T(8,128)(2,1)} %bitcast.5), custom_call_target="tpu_custom_call" | custom-call | tf_op jit(solution)/shard_map/pallas_call | solution.py:212
  34.6 0.7 %copy.4 = f32[256,2,4,32]{0,3,2,1:T(8,128)} copy(f32[256,2,4,32]{0,3,2,1:T(8,128)S(1)} %bitcast.3) | data formatting | bytes 524288

commit v7 on v6

--- a/solution.py
+++ b/solution.py
@@ -99,7 +99,7 @@
     def send_line(j, wait):
         def step(i, carry):
             nx = lax.div(i, 8) * 2 + lax.rem(x + i, 2)
-            ny = lax.rem(y + lax.div(lax.rem(i, 8), 2), NY)
+            ny = lax.rem(y + 4 - lax.div(lax.rem(i, 8), 2), NY)
 
             @pl.when((nx != x) | (ny != y))
             def _():

time: 35.7 us -> 35.1 us (0.983)
  Pallas kernels: 34.6 us -> 34.2 us
    pallas_call x1, Pallas kernels: 34.6 us -> 34.2 us  [on_device(): pl.pallas_call(exchange_kernel, out_shape=pltpu.VMEM((2, 4, 32, 256), F32...]
where the time goes in v7:
time: 35.1 us; the launch traced here: 34.9 us
  Pallas kernels  34.2 us (97%)
  local copies, waits for them, and re-layouts  0.71 us (2%)
    pallas_call x1, Pallas kernels, on_device(): pl.pallas_call(exchange_kernel, out_shape=pltpu.VMEM((2, 4, 32, 256), F32...  34.2 us
    unnamed x1, local copies, waits for them, and re-layouts  0.71 us

profile of v7, /device:TPU:1, one launch (start us, length us, event | category | flops | bytes accessed | tf_op | source)
XLA Modules:
  0.0 34.9 jit_solution(11763992244607882722)
XLA Ops:
  0.0 34.2 %shard_map.28 = f32[2,4,32,256]{3,2,1,0:T(8,128)S(1)} custom-call(bf16[2,256,512]{2,1,0:T(8,128)(2,1)} %bitcast.4, bf16[2,2,2,64,512]{4,3,2,1,0:T(8,128)(2,1)} %bitcast.5), custom_call_target="tpu_custom_call" | custom-call | tf_op jit(solution)/shard_map/pallas_call | solution.py:212
  34.2 0.7 %copy.4 = f32[256,2,4,32]{0,3,2,1:T(8,128)} copy(f32[256,2,4,32]{0,3,2,1:T(8,128)S(1)} %bitcast.3) | data formatting | bytes 524288

commit v8 on v7

--- a/solution.py
+++ b/solution.py
@@ -99,7 +99,7 @@
     def send_line(j, wait):
         def step(i, carry):
             nx = lax.div(i, 8) * 2 + lax.rem(x + i, 2)
-            ny = lax.rem(y + 4 - lax.div(lax.rem(i, 8), 2), NY)
+            ny = lax.rem(y + (1 if wait else 3) * lax.div(lax.rem(i, 8), 2), NY)
 
             @pl.when((nx != x) | (ny != y))
             def _():

time: 35.1 us -> 35.4 us (level); the launches traced: 34.9 us -> 34.9 us
  no operation moved by 1% of the time
where the time goes in v8:
time: 35.4 us; the launch traced here: 34.9 us
  Pallas kernels  34.1 us (96%)
  local copies, waits for them, and re-layouts  0.71 us (2%)
    pallas_call x1, Pallas kernels, on_device(): pl.pallas_call(exchange_kernel, out_shape=pltpu.VMEM((2, 4, 32, 256), F32...  34.1 us

profile of v8, /device:TPU:1, one launch (start us, length us, event | category | flops | bytes accessed | tf_op | source)
XLA Modules:
  0.0 34.9 jit_solution(13529474719654381384)
XLA Ops:
  0.0 34.1 %shard_map.28 = f32[2,4,32,256]{3,2,1,0:T(8,128)S(1)} custom-call(bf16[2,256,512]{2,1,0:T(8,128)(2,1)} %bitcast.4, bf16[2,2,2,64,512]{4,3,2,1,0:T(8,128)(2,1)} %bitcast.5), custom_call_target="tpu_custom_call" | custom-call | tf_op jit(solution)/shard_map/pallas_call | solution.py:212
  34.2 0.7 %copy.4 = f32[256,2,4,32]{0,3,2,1:T(8,128)} copy(f32[256,2,4,32]{0,3,2,1:T(8,128)S(1)} %bitcast.3) | data formatting | bytes 524288
